TPU v7x, 32 devices: a 4x4x1 block of a 4x4x8 slice. The times are simulated.
32 devices in a mesh: data: 1 (over z), expert: 32 (over y, x, core).
Axes of the slice: x: 4, y: 4, z: 1, core: 2. Of those that a mesh axis runs over, the one named last changes fastest.
The devices are a block of a 4x4x8 slice.
Arguments:
- tokens: bfloat16 [16384, 2048], P(('data', 'expert'))
- w_router: bfloat16 [2048, 64], replicated
- routes: int32 [16384, 6], P(('data', 'expert'))
- w_gate: bfloat16 [64, 2048, 1408], P('expert')
- w_up: bfloat16 [64, 2048, 1408], P('expert')
- w_down: bfloat16 [64, 1408, 2048], P('expert')
Outputs:
- output: bfloat16 [16384, 2048], P(('data', 'expert'))
All inputs are finite; a program needn't handle non-finite values.
Results may differ from a plain program's by a relative error of at most 0.00138.
Values are sent between devices in bfloat16 or wider.
A program may use at most 768 MiB of HBM per device.

v0:
```python
import jax
import jax.numpy as jnp
from jax import lax
from jax.sharding import PartitionSpec as P


def solution(mesh):
    group_size = mesh.shape['expert']
    row_spec = P(('data', 'expert'), None)
    expert_spec = P('expert', None, None)

    def device_step(tokens, w_router, routes, w_gate, w_up, w_down):
        tok_count, width = tokens.shape
        slots_per_tok = routes.shape[1]
        experts = w_router.shape[1]
        local_experts = w_gate.shape[0]
        capacity = 4 * tok_count * slots_per_tok // experts
        logits = jnp.dot(tokens, w_router, preferred_element_type=jnp.float32)
        gate_vals = jax.nn.softmax(jnp.take_along_axis(logits, routes, axis=1), axis=-1)
        flat_ids = routes.reshape(-1)
        onehot = (flat_ids[:, None] == jnp.arange(experts, dtype=jnp.int32)[None, :]).astype(jnp.int32)
        pair_rank = jnp.sum((jnp.cumsum(onehot, axis=0) - 1) * onehot, axis=1)
        slot_pos = flat_ids * capacity + pair_rank
        pair_tok = jnp.arange(tok_count * slots_per_tok, dtype=jnp.int32) // slots_per_tok
        slot_tok = jnp.full((experts * capacity,), tok_count, jnp.int32).at[slot_pos].set(pair_tok)
        send_rows = jnp.take(tokens, slot_tok, axis=0, mode='fill', fill_value=0)
        send_rows = send_rows.reshape(group_size, local_experts, capacity, width)
        recv_rows = lax.all_to_all(send_rows, 'expert', 0, 0, tiled=True)
        hidden = jax.nn.silu(jnp.einsum('secd,edf->secf', recv_rows, w_gate, preferred_element_type=jnp.float32)) * jnp.einsum('secd,edf->secf', recv_rows, w_up, preferred_element_type=jnp.float32)
        expert_out = jnp.einsum('secf,efd->secd', hidden.astype(jnp.bfloat16), w_down, preferred_element_type=jnp.float32).astype(jnp.bfloat16)
        back_rows = lax.all_to_all(expert_out, 'expert', 0, 0, tiled=True)
        pair_rows = jnp.take(back_rows.reshape(experts * capacity, width), slot_pos, axis=0)
        pair_rows = pair_rows.reshape(tok_count, slots_per_tok, width)
        combined = jnp.sum(pair_rows * gate_vals[:, :, None], axis=1)
        return combined.astype(jnp.bfloat16)

    return jax.shard_map(device_step, mesh=mesh, in_specs=(row_spec, P(None, None), row_spec, expert_spec, expert_spec, expert_spec), out_specs=row_spec, check_vma=False)
```

profile of v0, /device:TPU:103, one launch (start us, length us, event | category | flops | bytes accessed | tf_op | source)
XLA Modules:
  0.0 1865.4 jit_solution(17386808348432235898)
XLA Ops:
  0.0 1.0 copy.35
  1.0 0.2 eq.26
  1.4 0.7 broadcast_multiply_fusion
  2.1 0.9 fusion.15
  3.0 31.9 %reduce-window.6 = s32[64,24,128]{2,1,0:T(8,128)S(1)} reduce-window(s32[64,24,128]{2,1,0:T(8,128)} %fusion.15, s32[]{:T(128)} %constant.44.clone.1), window={size=1x1x128 pad=0_0x0_0x127_0}, to_apply=%region_0.0 | reduce-window | flops 24969216 | bytes 1572868 | tf_op jit(solution)/shard_map/reduce-window
  34.9 1.2 slice.14
  36.1 1.6 copy.51
  37.6 0.2 reduce-window.9
  37.8 1.2 add_add_fusion
  39.1 0.2 mul.40
  39.3 1.3 fusion.14
  40.7 0.6 copy-done.3
  41.3 0.6 copy-done.5
  41.9 11.8 scatter_custom_fusion
  53.8 60.6 %gather_fusion = bf16[12288,2048]{1,0:T(8,128)(2,1)} fusion(bf16[512,2048]{1,0:T(8,128)(2,1)S(1)} %copy-done, s32[12288]{0:T(1024)S(1)} %fusion.20), kind=kCustom, calls=%fused_computation | custom fusion | bytes 100712448 | tf_op jit(solution)/shard_map/jit(_take)/gather | solution.py:26
  114.5 33.7 %broadcast_select_fusion = bf16[32,2,192,2048]{3,2,1,0:T(8,128)(2,1)} fusion(bf16[32,2,192,2048]{3,2,1,0:T(8,128)(2,1)} %bitcast.78, pred[32,2,192]{2,1,0:T(4,128)(4,1)S(1)} %broadcast_in_dim.38), kind=kLoop, calls=%fused_computation.12 | loop fusion | flops 25165824 | bytes 100675584 | tf_op jit(solution)/shard_map/jit(_take)/select_n | solution.py:26
  148.2 618.2 %all_to_all.10 = bf16[32,2,192,2048]{3,2,1,0:T(8,128)(2,1)} all-to-all(bf16[32,2,192,2048]{3,2,1,0:T(8,128)(2,1)} %broadcast_select_fusion), channel_id=1, replica_groups=mesh['data'=1,'expert'=32] {'expert'}, dimensions={0} | all-to-all | bytes 100663296 | tf_op jit(solution)/shard_map/all_to_all | solution.py:28
  766.4 87.8 %fusion.4 = f32[2,32,192,1408]{3,2,1,0:T(8,128)} fusion(bf16[32,2,192,2048]{3,2,1,0:T(8,128)(2,1)} %all_to_all.10, bf16[2,2048,1408]{2,1,0:T(8,128)(2,1)} %param.10), kind=kOutput, calls=%fused_computation.13 | convolution fusion | flops 70866960384 | bytes 131072000 | tf_op jit(solution)/shard_map/secd,edf->secf/dot_general | solution.py:29
  854.3 99.3 %fusion.clone.4 = bf16[32,2,192,1408]{3,2,0,1:T(8,128)(2,1)} fusion(f32[2,32,192,1408]{3,2,1,0:T(8,128)} %fusion.4, bf16[32,2,192,2048]{3,2,1,0:T(8,128)(2,1)} %all_to_all.10, bf16[2,2048,1408]{2,1,0:T(8,128)(2,1)} %param.9), kind=kOutput, calls=%fused_computation.5.clone.clone.clone.1 | convolution fusion | flops 70970769408 | bytes 165675008 | tf_op jit(solution)/shard_map/secd,edf->secf/dot_general | solution.py:29
  953.5 87.2 %convert_bitcast_fusion = bf16[32,2,192,2048]{3,2,0,1:T(8,128)(2,1)} fusion(bf16[2,1408,2048]{2,1,0:T(8,128)(2,1)} %param.11, bf16[32,2,192,1408]{3,2,0,1:T(8,128)(2,1)} %fusion.clone.4), kind=kOutput, calls=%fused_computation.11 | convolution fusion | flops 70892126208 | bytes 96468992 | tf_op jit(solution)/shard_map/secf,efd->secd/dot_general | solution.py:30
  1040.7 33.5 %copy.44 = bf16[32,2,192,2048]{3,2,1,0:T(8,128)(2,1)} copy(bf16[32,2,192,2048]{3,2,0,1:T(8,128)(2,1)} %convert_bitcast_fusion) | data formatting | bytes 100663296 | tf_op jit(solution)/shard_map/convert_element_type | solution.py:30
  1074.2 9.4 all-to-all-start.1
  1083.7 0.2 reduce_sum.32
  1084.1 0.2 reshape.128
  1084.3 0.8 fusion.30
  1085.1 24.9 %gather_fusion.2 = f32[3072]{0:T(1024)S(1)} fusion(f32[512,64]{0,1:T(8,128)S(1)} %fusion.30, s32[3072]{0:T(1024)S(1)} %reshape.128), kind=kCustom, calls=%fused_computation.2 | custom fusion | bytes 49152 | tf_op jit(solution)/shard_map/jit(take_along_axis)/gather | solution.py:19
  1110.0 0.2 reshape.131
  1110.7 0.2 copy.40
  1110.9 641.7 %all-to-all-done.1 = bf16[32,2,192,2048]{3,2,1,0:T(8,128)(2,1)} async-done(((bf16[32,2,192,2048]{3,2,1,0:T(8,128)(2,1)}), bf16[32,2,192,2048]{3,2,1,0:T(8,128)(2,1)}, u32[]{:S(2)}, u32[]{:S(2)}) %all-to-all-start.1) | async-done | bytes 50331680 | tf_op jit(solution)/shard_map/all_to_all | solution.py:31
  1752.6 71.8 %gather_fusion.1 = bf16[3072,2048]{1,0:T(8,128)(2,1)} fusion(bf16[12288,2048]{1,0:T(8,128)(2,1)} %bitcast.15, s32[3072]{0:T(1024)S(1)} %broadcast_clamp_fusion), kind=kCustom, calls=%fused_computation.1 | custom fusion | bytes 25178112 | tf_op jit(solution)/shard_map/jit(_take)/gather | solution.py:32
  1824.4 20.4 %gather.19 = bf16[512,6,2048]{2,1,0:T(8,128)(2,1)} reshape(bf16[3072,2048]{1,0:T(8,128)(2,1)} %gather_fusion.1) | data formatting | bytes 25165824 | tf_op jit(solution)/shard_map/jit(_take)/gather | solution.py:32
  1844.8 20.6 %multiply_reduce_fusion = bf16[512,2048]{1,0:T(8,128)(2,1)} fusion(f32[512,6]{1,0:T(8,128)S(1)} %copy.47, bf16[512,6,2048]{2,1,0:T(8,128)(2,1)} %gather.19, pred[512,6]{1,0:T(8,128)(4,1)S(1)} %copy.40), kind=kLoop, calls=%fused_computation.17 | loop fusion | flops 24117248 | bytes 14695424 | tf_op jit(solution)/shard_map/reduce_sum | solution.py:34
  (29 shorter events, 1.1 us)
Async XLA Ops:
  0.0 53.8 %copy-start = (bf16[512,2048]{1,0:T(8,128)(2,1)S(1)}, bf16[512,2048]{1,0:T(8,128)(2,1)}, u32[]{:S(2)}) copy-start(bf16[512,2048]{1,0:T(8,128)(2,1)} %param.6) | copy-start | bytes 6291460
  40.7 0.6 copy-start.3
  41.3 0.6 copy-start.5
  1074.2 9.5 copy-start.4
  1074.2 9.7 copy-start.1
  1074.2 10.0 copy-start.2
  1074.2 678.3 %all-to-all-start.1 = ((bf16[32,2,192,2048]{3,2,1,0:T(8,128)(2,1)}), bf16[32,2,192,2048]{3,2,1,0:T(8,128)(2,1)}, u32[]{:S(2)}, u32[]{:S(2)}) async-start(bf16[32,2,192,2048]{3,2,1,0:T(8,128)(2,1)} %copy.44), calls=%async_computation.1 | async-start | bytes 100663296 | tf_op jit(solution)/shard_map/all_to_all | solution.py:31
  1085.0 25.8 %copy-start.6 = (s32[3072,1]{0,1:T(1,128)S(1)}, s32[3072,1]{0,1:T(1,128)}, u32[]{:S(2)}) copy-start(s32[3072,1]{0,1:T(1,128)} %copy-done.5) | copy-start | bytes 36868
where the time goes:
time: 1870 us
  waiting for transfers between devices  642 us (34%)
  blocking collectives  618 us (33%)
  matrix products  275 us (15%)
  local copies, waits for them, and re-layouts  230 us (12%)
  other arithmetic  90.7 us (5%)
    all_to_all x1, waiting for transfers between devices, device_step(): back_rows = lax.all_to_all(expert_out, 'expert', 0, 0, tiled=True)  642 us
    all_to_all x1, blocking collectives, device_step(): recv_rows = lax.all_to_all(send_rows, 'expert', 0, 0, tiled=True)  618 us
    dot_general x1, matrix products, device_step(): jnp.einsum('secd,edf->secf', recv_rows, w_gate, preferred_element_type=jn...  99.3 us
    gather x2, local copies, waits for them, and re-layouts, device_step(): jnp.take(back_rows.reshape(experts * capacity, width), slot_pos, axis=0)  92.2 us
    dot_general x1, matrix products, device_step(): jnp.einsum('secd,edf->secf', recv_rows, w_up, preferred_element_type=jnp....  87.8 us
    dot_general x1, matrix products, device_step(): jnp.einsum('secf,efd->secd', hidden.astype(jnp.bfloat16), w_down, preferr...  87.2 us
    gather x1, local copies, waits for them, and re-layouts, device_step(): send_rows = jnp.take(tokens, slot_tok, axis=0, mode='fill', fill_value=0)  60.6 us
  transfers between devices with their start and end apart: 1, of which 1 were waited for; matrix products, arithmetic and copies ran while one was open for 1% of the time, Pallas kernels for 0%

commit v1 on v0

v1 whole, which is shorter than its diff:
```python
import functools
import math

import jax
import jax.numpy as jnp
from jax import lax
from jax.experimental import pallas as pl
from jax.experimental.pallas import tpu as pltpu
from jax.sharding import PartitionSpec as P

BF16 = jnp.bfloat16
F32 = jnp.float32
LANE = 128
CHUNK = 256
RINGS = 4
HOT = 4
SLOTS = 4
CORES = 2


def stream_kernel(side, n_real, n_all, local, sel_ref, wg, wu, wd, log, cand, recv, send,
                  cand_sem, pair_sem, recv_sem, ring_sem, log_sem, sib_sem, sib_recv_sem, credit, pair_credit):
    me = lax.axis_index('expert')
    core = me % CORES
    chip = me // CORES
    y, x = chip // side, chip % side
    sib = chip * CORES + 1 - core

    turn = ((x + y) % side) // (side - 1)
    dx = (1 - core) * (1 - turn) + core * turn
    ahead = (((y + 1 - dx) % side) * side + (x + dx) % side) * CORES + core
    turn_b = ((x + y + side - 1) % side) // (side - 1)
    dx_b = (1 - core) * (1 - turn_b) + core * turn_b
    behind = (((y + dx_b - 1 + side) % side) * side + (x + side - dx_b) % side) * CORES + core
    down = (ahead, behind)
    up = (behind, ahead)

    for k in range(HOT):
        for d in range(2):
            recv[SLOTS - 1, d, k] = jnp.zeros((CHUNK, LANE), BF16)

    barrier = pltpu.get_barrier_semaphore()
    for other in (ahead, behind, sib):
        pl.semaphore_signal(barrier, inc=1, device_id={'expert': other}, device_id_type=pl.DeviceIdType.MESH)
    pl.semaphore_wait(barrier, 3)

    per_mat = n_real // 3

    def fetch_from(p, make):
        kind = p // per_mat
        within = p % per_mat
        j, b = within // 2, within % 2

        def rows_of(w):
            for to_sib in (0, 1):
                owner_core = core if to_sib == 0 else 1 - core
                for d in range(2):
                    blk = (owner_core * 2 + d) * 2 + b
                    for le in range(local):
                        make(le, d, to_sib, w.at[le, pl.ds(pl.multiple_of(blk * CHUNK, CHUNK), CHUNK),
                                                 pl.ds(pl.multiple_of(j * LANE, LANE), LANE)], None)

        @pl.when(kind == 0)
        def _():
            rows_of(wg)

        @pl.when(kind == 1)
        def _():
            rows_of(wu)

        @pl.when(kind == 2)
        def _():
            for to_sib in (0, 1):
                owner_core = core if to_sib == 0 else 1 - core
                for d in range(2):
                    blk = (owner_core * 2 + d) * 2 + b
                    for le in range(local):
                        for part in range(2):
                            make(le, d, to_sib, wd.at[le, pl.ds(pl.multiple_of(j * LANE, LANE), LANE),
                                                      pl.ds(pl.multiple_of(blk * CHUNK + part * LANE, LANE), LANE)], part)

    def prefetch(p):
        slot = p % SLOTS

        @pl.when(p >= SLOTS)
        def _():
            pl.semaphore_wait(pair_credit, 1)
            for d in range(2):
                for le in range(local):
                    wait_pair(slot, d, le)

        def make(le, d, to_sib, src, part):
            dst = cand.at[slot, d, core * local + le]
            if part is not None:
                dst = dst.at[pl.ds(part * LANE, LANE)]
            if to_sib:
                pltpu.make_async_remote_copy(src_ref=src, dst_ref=dst, send_sem=pair_sem.at[slot, d, le],
                                             recv_sem=cand_sem.at[slot, d, core * local + le],
                                             device_id={'expert': sib}, device_id_type=pl.DeviceIdType.MESH).start()
            else:
                pltpu.make_async_copy(src, dst, cand_sem.at[slot, d, core * local + le]).start()

        fetch_from(p, make)

    def wait_pair(slot, d, le):
        one = cand.at[slot, d, core * local + le]
        pltpu.make_async_copy(one, one, pair_sem.at[slot, d, le]).wait()

    def ring_copy(slot, d, k):
        return pltpu.make_async_remote_copy(src_ref=send.at[slot, d, k], dst_ref=recv.at[slot, d, k],
                                            send_sem=ring_sem.at[slot, d, k], recv_sem=recv_sem.at[slot, d, k],
                                            device_id={'expert': down[d]}, device_id_type=pl.DeviceIdType.MESH)

    def log_copy(slot, d, s):
        return pltpu.make_async_copy(send.at[slot, d], log.at[core * 2 + d, s], log_sem.at[slot, d])

    def sib_copy(slot, d, s):
        return pltpu.make_async_remote_copy(src_ref=send.at[slot, d], dst_ref=log.at[core * 2 + d, s],
                                            send_sem=sib_sem.at[slot, d], recv_sem=sib_recv_sem.at[d],
                                            device_id={'expert': sib}, device_id_type=pl.DeviceIdType.MESH)

    def step(s, own):
        slot = s % SLOTS
        before = (s + SLOTS - 1) % SLOTS
        if own:
            @pl.when(s + 2 < n_real)
            def _():
                prefetch(s + 2)
            for d in range(2):
                for e in range(CORES * local):
                    one = cand.at[slot, d, e]
                    pltpu.make_async_copy(one, one, cand_sem.at[slot, d, e]).wait()

        @pl.when((s >= SLOTS - 1) & (s <= n_all - 2))
        def _():
            for d in range(2):
                pl.semaphore_wait(credit.at[d], 1)

        @pl.when(s >= SLOTS)
        def _():
            for d in range(2):
                log_copy(slot, d, s).wait()
                sib_copy(slot, d, s).wait_send()
                for k in range(HOT):
                    ring_copy(slot, d, k).wait_send()

        for k in range(HOT):
            for d in range(2):
                @pl.when(s >= 1)
                def _():
                    ring_copy(before, d, k).wait_recv()
                value = recv[before, d, k]
                if own:
                    pick = sel_ref[k]
                    for e in range(CORES * local):
                        value = jnp.where(pick == e + 1, cand[slot, d, e], value)
                send[slot, d, k] = value

                @pl.when(s <= n_all - 2)
                def _():
                    ring_copy(slot, d, k).start()
        for d in range(2):
            log_copy(slot, d, s).start()
            sib_copy(slot, d, s).start()

        @pl.when(s <= n_all - SLOTS - 1)
        def _():
            for d in range(2):
                pl.semaphore_signal(credit.at[d], inc=1, device_id={'expert': up[d]},
                                    device_id_type=pl.DeviceIdType.MESH)
        if own:
            @pl.when(s <= n_real - SLOTS - 1)
            def _():
                pl.semaphore_signal(pair_credit, inc=1, device_id={'expert': sib},
                                    device_id_type=pl.DeviceIdType.MESH)

    def first(p, carry):
        prefetch(p)
        return carry

    def with_own(s, carry):
        step(s, True)
        return carry

    def without_own(s, carry):
        step(s, False)
        return carry

    lax.fori_loop(0, 2, first, 0)
    lax.fori_loop(0, n_real, with_own, 0)
    lax.fori_loop(n_real, n_all, without_own, 0)

    for back in range(SLOTS):
        slot = (n_all - 1 - back) % SLOTS
        for d in range(2):
            log_copy(slot, d, 0).wait()
            sib_copy(slot, d, 0).wait_send()
            if back > 0:
                for k in range(HOT):
                    ring_copy(slot, d, k).wait_send()
        slot = (n_real - 1 - back) % SLOTS
        for d in range(2):
            for le in range(local):
                wait_pair(slot, d, le)
    for d in range(2):
        theirs = log.at[(1 - core) * 2 + d]
        pltpu.make_async_copy(theirs, theirs, sib_recv_sem.at[d]).wait()


def stream_weights(group_size, sel, w_gate, w_up, w_down):
    local, width, ff = w_gate.shape
    side = math.isqrt(group_size // CORES)
    n_real = 3 * (width // CHUNK) * (ff // LANE) // RINGS
    n_all = n_real + side * side - 1
    any_spec = pl.BlockSpec(memory_space=pl.ANY)
    return pl.pallas_call(
        functools.partial(stream_kernel, side, n_real, n_all, local),
        out_shape=jax.ShapeDtypeStruct((RINGS, n_all, HOT, CHUNK, LANE), BF16),
        in_specs=[pl.BlockSpec(memory_space=pltpu.SMEM), any_spec, any_spec, any_spec],
        out_specs=any_spec,
        scratch_shapes=[
            pltpu.VMEM((SLOTS, 2, CORES * local, CHUNK, LANE), BF16),
            pltpu.VMEM((SLOTS, 2, HOT, CHUNK, LANE), BF16),
            pltpu.VMEM((SLOTS, 2, HOT, CHUNK, LANE), BF16),
            pltpu.SemaphoreType.DMA((SLOTS, 2, CORES * local)),
            pltpu.SemaphoreType.DMA((SLOTS, 2, local)),
            pltpu.SemaphoreType.DMA((SLOTS, 2, HOT)),
            pltpu.SemaphoreType.DMA((SLOTS, 2, HOT)),
            pltpu.SemaphoreType.DMA((SLOTS, 2)),
            pltpu.SemaphoreType.DMA((SLOTS, 2)),
            pltpu.SemaphoreType.DMA((2,)),
            pltpu.SemaphoreType.REGULAR((2,)),
            pltpu.SemaphoreType.REGULAR,
        ],
        compiler_params=pltpu.CompilerParams(collective_id=1, has_side_effects=True),
        cost_estimate=pl.CostEstimate(flops=0, bytes_accessed=700_000_000, transcendentals=0),
        name='stream_weights',
    )(sel, w_gate, w_up, w_down)


def hot_kernel(parts, offs_ref, x_ref, *refs):
    gates, ups, downs = refs[:parts], refs[parts:2 * parts], refs[2 * parts:3 * parts]
    out_ref, acc = refs[3 * parts], refs[3 * parts + 1]
    j = pl.program_id(1)

    @pl.when(j == 0)
    def _():
        acc[...] = jnp.zeros_like(acc)

    ab = None
    for i in range(parts):
        both = jnp.concatenate([gates[i][...], ups[i][...]], axis=1)
        term = jnp.dot(x_ref[:, i * CHUNK:(i + 1) * CHUNK], both, preferred_element_type=F32)
        ab = term if ab is None else ab + term
    hidden = (jax.nn.silu(ab[:, :LANE]) * ab[:, LANE:]).astype(BF16)
    for i in range(parts):
        both = jnp.concatenate([downs[i][:LANE], downs[i][LANE:]], axis=1)
        acc[:, i * CHUNK:(i + 1) * CHUNK] += jnp.dot(hidden, both, preferred_element_type=F32)

    @pl.when(j == pl.num_programs(1) - 1)
    def _():
        out_ref[...] = acc[...].astype(BF16)


def hot_experts(offs, x_hot, log, ff):
    _, rows, width = x_hot.shape
    parts = width // CHUNK
    blocks = ff // LANE

    def piece(mat, i):
        ring, b = i // 2, i % 2
        return pl.BlockSpec((None, None, None, CHUNK, LANE),
                            lambda k, j, o: (ring, o[k * RINGS + ring] + mat * 2 * blocks + 2 * j + b, k, 0, 0))

    row_spec = pl.BlockSpec((None, rows, width), lambda k, j, o: (k, 0, 0))
    return pl.pallas_call(
        functools.partial(hot_kernel, parts),
        out_shape=jax.ShapeDtypeStruct((HOT, rows, width), BF16),
        grid_spec=pltpu.PrefetchScalarGridSpec(
            num_scalar_prefetch=1, grid=(HOT, blocks),
            in_specs=[row_spec] + [piece(m, i) for m in range(3) for i in range(parts)],
            out_specs=row_spec,
            scratch_shapes=[pltpu.VMEM((rows, width), F32)]),
        compiler_params=pltpu.CompilerParams(dimension_semantics=('arbitrary', 'arbitrary')),
        cost_estimate=pl.CostEstimate(flops=6 * HOT * rows * width * ff, bytes_accessed=6 * HOT * width * ff,
                                      transcendentals=0),
        name='hot_experts',
    )(offs, x_hot, *([log] * (3 * parts)))


def split3(v):
    hi = lax.reduce_precision(v, 8, 7)
    mid = lax.reduce_precision(v - hi, 8, 7)
    low = lax.reduce_precision(v - hi - mid, 8, 7)
    return [hi.astype(BF16), mid.astype(BF16), low.astype(BF16)]


def weighted(pos, cap, gate_parts, rows):
    toks, count = pos.shape
    hit = pos[:, :, None] == jnp.arange(cap, dtype=jnp.int32)[None, None, :]
    mats = [jnp.where(hit, g[:, :, None], jnp.zeros((), BF16)).reshape(toks, count * cap) for g in gate_parts]
    out = jnp.dot(jnp.concatenate(mats, axis=0), rows, preferred_element_type=F32)
    return out[:toks] + out[toks:2 * toks] + out[2 * toks:]


def solution(mesh):
    group_size = mesh.shape['expert']
    row_spec = P(('data', 'expert'), None)
    expert_spec = P('expert', None, None)
    side = math.isqrt(group_size // CORES)
    ring_len = side * side

    def device_step(tokens, w_router, routes, w_gate, w_up, w_down):
        toks, width = tokens.shape
        picks = routes.shape[1]
        experts = w_router.shape[1]
        local, _, ff = w_gate.shape
        capacity = 4 * toks * picks // experts
        cold_cap = capacity // 3
        hot_cap = capacity - cold_cap

        logits = jnp.dot(tokens, w_router, preferred_element_type=F32)
        ids = jnp.arange(experts, dtype=jnp.int32)
        mask = jnp.any(routes[:, :, None] == ids[None, None, :], axis=1)
        top = jnp.max(jnp.where(mask, logits, -jnp.inf), axis=1, keepdims=True)
        raised = jnp.where(mask, jnp.exp(logits - top), 0.0)
        gates = raised / jnp.sum(raised, axis=1, keepdims=True)
        gate_parts = split3(gates)

        order = jnp.arange(toks, dtype=jnp.int32)
        earlier = (order[None, :] < order[:, None]).astype(BF16)
        rank = jnp.dot(earlier, mask.astype(BF16), preferred_element_type=F32).astype(jnp.int32)
        pos = jnp.where(mask, rank, -1)
        counts = jnp.sum(mask.astype(jnp.int32), axis=0)

        pos_t = pos.T.reshape(group_size, local, toks)
        slots = jnp.arange(cold_cap, dtype=jnp.int32)
        received = []
        for le in range(local):
            pick_rows = (pos_t[:, le, None, :] == slots[None, :, None]).astype(BF16).reshape(group_size * cold_cap, toks)
            rows = jnp.dot(pick_rows, tokens, preferred_element_type=F32).astype(BF16)
            received.append(lax.all_to_all(rows.reshape(group_size, cold_cap, width), 'expert', 0, 0, tiled=True)
                            .reshape(group_size * cold_cap, width))

        most = lax.pmax(counts, 'expert')
        is_hot = most > cold_cap
        hot_place = jnp.cumsum(is_hot.astype(jnp.int32)) - 1
        n_hot = jnp.sum(is_hot.astype(jnp.int32))
        my_chip = lax.axis_index('expert') // CORES
        my_y, my_x = my_chip // side, my_chip % side
        ring_a = side * my_y + (my_x + my_y) % side
        ring_b = side * my_x + (my_x + my_y) % side

        def hot_pass(batch):
            want = batch * HOT + jnp.arange(HOT, dtype=jnp.int32)
            match = is_hot[None, :] & (hot_place[None, :] == want[:, None])
            there = jnp.any(match, axis=1)
            hot_id = jnp.sum(jnp.where(match, ids[None, :], 0), axis=1)
            chip = hot_id // (local * CORES)
            sel = jnp.where(there & (chip == my_chip), 1 + hot_id % (local * CORES), 0)
            cy, cx = chip // side, chip % side
            root_a = side * cy + (cx + cy) % side
            root_b = side * cx + (cx + cy) % side
            offs = jnp.stack([(ring_a - root_a) % ring_len, (root_a - ring_a) % ring_len,
                              (ring_b - root_b) % ring_len, (root_b - ring_b) % ring_len], axis=1).reshape(-1)
            log = stream_weights(group_size, sel, w_gate, w_up, w_down)
            col = jnp.sum(jnp.where(match[:, None, :], pos[None, :, :] - cold_cap, 0), axis=2)
            col = jnp.where(there[:, None], col, -1)
            hit = (col[:, None, :] == jnp.arange(hot_cap, dtype=jnp.int32)[None, :, None]).astype(BF16)
            x_hot = jnp.dot(hit.reshape(HOT * hot_cap, toks), tokens, preferred_element_type=F32).astype(BF16)
            o_hot = hot_experts(offs, x_hot.reshape(HOT, hot_cap, width), log, ff)
            g_hot = jnp.sum(jnp.where(match[:, None, :], gates[None, :, :], 0.0), axis=2)
            return weighted(col.T, hot_cap, split3(g_hot.T), o_hot.reshape(HOT * hot_cap, width))

        total = hot_pass(jnp.int32(0))
        for le in range(local):
            rows = received[le]
            hidden = jax.nn.silu(jnp.dot(rows, w_gate[le], preferred_element_type=F32)) * jnp.dot(
                rows, w_up[le], preferred_element_type=F32)
            out = jnp.dot(hidden.astype(BF16), w_down[le], preferred_element_type=F32).astype(BF16)
            back = lax.all_to_all(out.reshape(group_size, cold_cap, width), 'expert', 0, 0, tiled=True)
            pos_le = pos.reshape(toks, group_size, local)[:, :, le]
            total = total + weighted(pos_le, cold_cap, [g.reshape(toks, group_size, local)[:, :, le] for g in gate_parts],
                                     back.reshape(group_size * cold_cap, width))

        def more(state):
            return state[0] * HOT < n_hot

        def again(state):
            return state[0] + 1, state[1] + hot_pass(state[0])

        _, total = lax.while_loop(more, again, (jnp.int32(1), total))
        return total.astype(BF16)

    return jax.shard_map(device_step, mesh=mesh,
                         in_specs=(row_spec, P(None, None), row_spec, expert_spec, expert_spec, expert_spec),
                         out_specs=row_spec, check_vma=False)
```

time: 1870 us -> 885 us (0.47)
  waiting for transfers between devices: 642 us -> 124 us
  blocking collectives: 618 us -> 147 us
  Pallas kernels: 0 us -> 367 us
  local copies, waits for them, and re-layouts: 230 us -> 6.7 us
  matrix products: 275 us -> 177 us
  other arithmetic: 90.7 us -> 29.5 us
    all_to_all x1 -> x0, blocking collectives: 618 us -> none  [device_step(): recv_rows = lax.all_to_all(send_rows, 'expert', 0, 0, tiled=True)]
    all_to_all x1 -> x4, waiting for transfers between devices: 642 us -> 124 us  [the longest x2 64 us: device_step(): lax.all_to_all(out.reshape(group_size, cold_cap, width), 'expert', 0, 0,...]
    pallas_call x0 -> x2, Pallas kernels: none -> 367 us  [the longest x1 304 us: stream_weights(): pl.pallas_call(functools.partial(stream_kernel, side, n_real, n_all, loca...]
    gather x8 -> x0, local copies, waits for them, and re-layouts: 178 us -> none  [the longest x2 92.2 us: device_step(): jnp.take(back_rows.reshape(experts * capacity, width), slot_pos, axis=0)]
    pmax x0 -> x1, blocking collectives: none -> 147 us  [device_step(): most = lax.pmax(counts, 'expert')]
    dot_general x4 -> x12, matrix products: 275 us -> 177 us  [the longest x2 70.3 us: device_step(): jnp.dot(hidden.astype(BF16), w_down[le], preferred_element_type=F32)]
    convert_element_type x1 -> x3, local copies, waits for them, and re-layouts: 33.5 us -> 0.53 us  [split3(): return [hi.astype(BF16), mid.astype(BF16), low.astype(BF16)]]
    another operation x2, other arithmetic: 32.1 us -> 0.11 us
  transfers between devices with their start and end apart: 1 -> 4, of which waited for: 1 -> 3; matrix products, arithmetic and copies ran while one was open for 1% -> 19% of each run, Pallas kernels for 0% -> 42%
where the time goes in v1:
time: 885 us; the launch traced here: 877 us
  Pallas kernels  367 us (41%)
  matrix products  177 us (20%)
  blocking collectives  147 us (17%)
  waiting for transfers between devices  124 us (14%)
  other arithmetic  29.5 us (3%)
  starting transfers between devices  23.8 us (3%)
    pallas_call x1, Pallas kernels, stream_weights(): pl.pallas_call(functools.partial(stream_kernel, side, n_real, n_all, loca...  304 us
    pmax x1, blocking collectives, device_step(): most = lax.pmax(counts, 'expert')  147 us
    dot_general x2, matrix products, device_step(): jnp.dot(hidden.astype(BF16), w_down[le], preferred_element_type=F32)  70.3 us
    all_to_all x2, waiting for transfers between devices, device_step(): lax.all_to_all(out.reshape(group_size, cold_cap, width), 'expert', 0, 0,...  64 us
    pallas_call x1, Pallas kernels, hot_experts(): pl.pallas_call(functools.partial(hot_kernel, parts), out_shape=jax.ShapeD...  62.7 us
    all_to_all x2, waiting for transfers between devices, device_step(): lax.all_to_all(rows.reshape(group_size, cold_cap, width), 'expert', 0, 0,...  60.2 us
    dot_general x3, matrix products, weighted(): jnp.dot(jnp.concatenate(mats, axis=0), rows, preferred_element_type=F32)  50.1 us
    dot_general x2, matrix products, device_step(): jnp.dot(rows, w_gate[le], preferred_element_type=F32)  37.1 us
  transfers between devices with their start and end apart: 4, of which 3 were waited for; matrix products, arithmetic and copies ran while one was open for 19% of the time, Pallas kernels for 42%

profile of v1, /device:TPU:103, one launch (start us, length us, event | category | flops | bytes accessed | tf_op | source)
XLA Modules:
  0.0 876.6 jit_solution(5265331088767955674)
XLA Ops:
  0.0 0.9 fusion.66
  0.9 0.9 broadcast_add_fusion.1
  2.1 1.3 bitcast_compare_fusion.4
  3.4 8.3 convolution_convert_fusion.4
  11.8 8.0 all-to-all-start
  19.8 0.7 reshape.920
  20.7 147.1 %pmax.7 = s32[64]{0:T(128)S(1)} all-reduce(s32[64]{0:T(128)S(1)} %convert_reduce_fusion), channel_id=1, replica_groups=mesh['data'=1,'expert'=32] {'expert'}, use_global_device_ids=true, to_apply=%region_2.3 | all-reduce | flops 64 | bytes 512 | tf_op jit(solution)/shard_map/pmax | solution.py:345
  170.1 304.4 %stream_weights.2.refs_0_.refs_1_.refs_2_.refs_3_.refs_4_.refs_5_.refs_6_.refs_7_.refs_8_.refs_9_.refs_10_.refs_11_.refs_12_.refs_13_.refs_14_.refs_15_.refs_16_.refs_17_.refs_18_.refs_19_.refs_20_.refs_21_.refs_22_.refs_23_ = bf16[4,81,4,256,128]{4,3,2,1,0:T(8,128)(2,1)} custom-call(s32[4]{0:T(128)} %and_select_fusion.12.sel_ref, ...), custom_call_target="tpu_custom_call" | custom-call | bytes 700000000 | tf_op jit(solution)/shard_map/stream_weights/pallas_call | solution.py:216
  474.5 0.8 select_reduce_fusion.4
  475.4 0.7 reduce-precision_convert_fusion.3
  476.1 6.6 convolution_convert_fusion.2
  482.7 7.4 all-to-all-start.2
  490.1 18.5 %fusion.39 = f32[2048,1408]{1,0:T(8,128)} fusion(bf16[2048,2048]{1,0:T(8,128)(2,1)} %bitcast.18, bf16[2,2048,1408]{2,1,0:T(8,128)(2,1)} %wg.1), kind=kOutput, calls=%fused_computation.96 | convolution fusion | flops 11811160064 | bytes 25690112 | tf_op jit(solution)/shard_map/dot_general | solution.py:378
  508.6 35.1 %convolution_convert_fusion.3 = bf16[2048,2048]{1,0:T(8,128)(2,1)} fusion(f32[2048,1408]{1,0:T(8,128)} %fusion.39, bf16[2048,2048]{1,0:T(8,128)(2,1)} %bitcast.18, bf16[2,1408,2048]{2,1,0:T(8,128)(2,1)} %wd.1, bf16[2,2048,1408]{2,1,0:T(8,128)(2,1)} %wu.1), kind=kOutput, calls=%fused_computation.76 | convolution fusion | flops 23643815936 | bytes 39845888 | tf_op jit(solution)/shard_map/dot_general | solution.py:380
  543.7 60.2 %all-to-all-done.2 = bf16[32,64,2048]{2,1,0:T(8,128)(2,1)} async-done(((bf16[32,64,2048]{2,1,0:T(8,128)(2,1)}), bf16[32,64,2048]{2,1,0:T(8,128)(2,1)}, u32[]{:S(2)}, u32[]{:S(2)}) %all-to-all-start.2) | async-done | bytes 8388640 | tf_op jit(solution)/shard_map/all_to_all | solution.py:342
  604.0 4.1 all-to-all-start.1
  608.1 18.5 %fusion.34 = f32[2048,1408]{1,0:T(8,128)} fusion(bf16[2048,2048]{1,0:T(8,128)(2,1)} %bitcast.33, bf16[2,2048,1408]{2,1,0:T(8,128)(2,1)} %wg.1), kind=kOutput, calls=%fused_computation.92 | convolution fusion | flops 11811160064 | bytes 25690112 | tf_op jit(solution)/shard_map/dot_general | solution.py:378
  626.6 35.2 %convolution_convert_fusion.1 = bf16[2048,2048]{1,0:T(8,128)(2,1)} fusion(f32[2048,1408]{1,0:T(8,128)} %fusion.34, bf16[2048,2048]{1,0:T(8,128)(2,1)} %bitcast.33, bf16[2,1408,2048]{2,1,0:T(8,128)(2,1)} %wd.1, bf16[2,2048,1408]{2,1,0:T(8,128)(2,1)} %wu.1), kind=kOutput, calls=%fused_computation.74 | convolution fusion | flops 23643815936 | bytes 39845888 | tf_op jit(solution)/shard_map/dot_general | solution.py:380
  661.8 59.4 %all-to-all-done.1 = bf16[32,64,2048]{2,1,0:T(8,128)(2,1)} async-done(((bf16[32,64,2048]{2,1,0:T(8,128)(2,1)}), bf16[32,64,2048]{2,1,0:T(8,128)(2,1)}, u32[]{:S(2)}, u32[]{:S(2)}) %all-to-all-start.1) | async-done | bytes 8388640 | tf_op jit(solution)/shard_map/all_to_all | solution.py:381
  721.2 4.3 all-to-all-start.3
  727.7 5.4 fusion.58
  734.4 1.3 eq.302
  735.7 1.1 bitcast_select_fusion.5
  738.0 1.2 bitcast_select_fusion.4
  739.2 2.6 convolution_convert_fusion.5
  741.8 62.7 %hot_experts.6 = bf16[4,128,2048]{2,1,0:T(8,128)(2,1)} custom-call(s32[16]{0:T(128)} %reshape.917.offs_ref, bf16[4,128,2048]{2,1,0:T(8,128)(2,1)} %bitcast.283, ...), custom_call_target="tpu_custom_call" | custom-call | flops 8858370048 | bytes 69206016 | tf_op jit(solution)/shard_map/hot_experts/pallas_call | solution.py:276
  804.6 9.8 %fusion.59 = f32[1536,2048]{1,0:T(8,128)} fusion(bf16[512,2048]{1,0:T(8,128)(2,1)} %bitcast.282, bf16[512,512]{1,0:T(8,128)(2,1)S(1)} %copy-done.19, bf16[512,512]{1,0:T(8,128)(2,1)S(1)} %copy-done.18, bf16[512,512]{1,0:T(8,128)(2,1)S(1)} %copy-done.17), kind=kOutput, calls=%fused_computation.125 | convolution fusion | flops 3225944064 | bytes 16252928 | tf_op jit(solution)/shard_map/dot_general | solution.py:302
  814.4 19.5 %fusion.19 = f32[1536,2048]{1,0:T(8,128)} fusion(bf16[2048,2048]{1,0:T(8,128)(2,1)} %bitcast.23, bf16[512,2048]{0,1:T(8,128)(2,1)S(1)} %copy-done.12, bf16[512,2048]{0,1:T(8,128)(2,1)S(1)} %copy-done.13, bf16[512,2048]{0,1:T(8,128)(2,1)S(1)} %copy-done.11), kind=kOutput, calls=%fused_computation.78 | convolution fusion | flops 12903776256 | bytes 27262976 | tf_op jit(solution)/shard_map/dot_general | solution.py:302
  833.9 4.6 all-to-all-done.3
  838.6 20.8 %fusion.25 = f32[1536,2048]{1,0:T(8,128)} fusion(bf16[2048,2048]{1,0:T(8,128)(2,1)} %bitcast.38, bf16[512,2048]{0,1:T(8,128)(2,1)} %get-tuple-element.376, bf16[512,2048]{0,1:T(8,128)(2,1)} %get-tuple-element.375, bf16[512,2048]{0,1:T(8,128)(2,1)} %get-tuple-element.377), kind=kOutput, calls=%fused_computation.84 | convolution fusion | flops 12903776256 | bytes 27262976 | tf_op jit(solution)/shard_map/dot_general | solution.py:302
  859.4 12.5 %fusion.51 = f32[512,2048]{1,0:T(8,128)} fusion(f32[1536,2048]{1,0:T(8,128)} %fusion.25, f32[1536,2048]{1,0:T(8,128)} %fusion.19, f32[1536,2048]{1,0:T(8,128)S(1)} %copy-done.2), kind=kLoop, calls=%fused_computation.107 | loop fusion | flops 8388608 | bytes 41943040 | tf_op jit(solution)/shard_map/add | solution.py:383
  872.5 3.9 convert_element_type.104
  (105 shorter events, 7.8 us)
Async XLA Ops:
  0.0 474.5 %copy-start = (bf16[2048,64]{0,1:T(8,128)(2,1)S(1)}, bf16[2048,64]{0,1:T(8,128)(2,1)}, u32[]{:S(2)}) copy-start(bf16[2048,64]{0,1:T(8,128)(2,1)} %param.9) | copy-start | bytes 786436
  1.8 18.0 %copy-start.5 = (s32[512,64]{0,1:T(8,128)}, s32[512,64]{0,1:T(8,128)S(1)}, u32[]{:S(2)}) copy-start(s32[512,64]{0,1:T(8,128)S(1)} %get-tuple-element.517) | copy-start | bytes 393220
  1.9 9.9 %copy-start.28 = (s32[2048]{0:T(1024)}, s32[2048]{0:T(1024)S(1)}, u32[]{:S(2)}) copy-start(s32[2048]{0:T(1024)S(1)} %eq.318) | copy-start | bytes 24580
  11.8 471.0 %all-to-all-start = ((bf16[32,64,2048]{2,1,0:T(8,128)(2,1)}), bf16[32,64,2048]{2,1,0:T(8,128)(2,1)}, u32[]{:S(2)}, u32[]{:S(2)}) async-start(bf16[32,64,2048]{2,1,0:T(8,128)(2,1)} %bitcast.276), calls=%async_computation | async-start | bytes 16777216 | tf_op jit(solution)/shard_map/all_to_all | solution.py:342
  168.2 1.3 copy-start.33
  168.5 1.0 copy-start.30
  168.7 0.9 copy-start.36
  168.7 0.9 copy-start.38
  170.1 304.4 %copy-start.8 = (bf16[512,2048]{1,0:T(8,128)(2,1)S(1)}, bf16[512,2048]{1,0:T(8,128)(2,1)}, u32[]{:S(2)}) copy-start(bf16[512,2048]{1,0:T(8,128)(2,1)} %param.8) | copy-start | bytes 6291460
  482.7 121.3 %all-to-all-start.2 = ((bf16[32,64,2048]{2,1,0:T(8,128)(2,1)}), bf16[32,64,2048]{2,1,0:T(8,128)(2,1)}, u32[]{:S(2)}, u32[]{:S(2)}) async-start(bf16[32,64,2048]{2,1,0:T(8,128)(2,1)} %bitcast.279), calls=%async_computation.2 | async-start | bytes 16777216 | tf_op jit(solution)/shard_map/all_to_all | solution.py:342
  604.0 117.2 %all-to-all-start.1 = ((bf16[32,64,2048]{2,1,0:T(8,128)(2,1)}), bf16[32,64,2048]{2,1,0:T(8,128)(2,1)}, u32[]{:S(2)}, u32[]{:S(2)}) async-start(bf16[32,64,2048]{2,1,0:T(8,128)(2,1)} %bitcast.278), calls=%async_computation.1 | async-start | bytes 16777216 | tf_op jit(solution)/shard_map/all_to_all | solution.py:381
  721.2 4.4 copy-start.3
  721.2 4.4 copy-start.39
  721.2 4.7 copy-start.25
  721.2 4.8 copy-start.37
  721.2 5.6 copy-start.22
  721.2 6.3 copy-start.16
  721.2 6.4 copy-start.29
  721.2 117.3 %all-to-all-start.3 = ((bf16[32,64,2048]{2,1,0:T(8,128)(2,1)}), bf16[32,64,2048]{2,1,0:T(8,128)(2,1)}, u32[]{:S(2)}, u32[]{:S(2)}) async-start(bf16[32,64,2048]{2,1,0:T(8,128)(2,1)} %bitcast.277), calls=%async_computation.3 | async-start | bytes 16777216 | tf_op jit(solution)/shard_map/all_to_all | solution.py:381
  727.7 5.4 copy-start.41
  733.1 6.1 copy-start.9
  741.8 62.7 %copy-start.17 = (bf16[512,512]{1,0:T(8,128)(2,1)S(1)}, bf16[512,512]{1,0:T(8,128)(2,1)}, u32[]{:S(2)}) copy-start(bf16[512,512]{1,0:T(8,128)(2,1)} %get-tuple-element.337) | copy-start | bytes 1572868
  741.8 62.7 %copy-start.18 = (bf16[512,512]{1,0:T(8,128)(2,1)S(1)}, bf16[512,512]{1,0:T(8,128)(2,1)}, u32[]{:S(2)}) copy-start(bf16[512,512]{1,0:T(8,128)(2,1)} %get-tuple-element.352) | copy-start | bytes 1572868
  741.8 62.7 %copy-start.19 = (bf16[512,512]{1,0:T(8,128)(2,1)S(1)}, bf16[512,512]{1,0:T(8,128)(2,1)}, u32[]{:S(2)}) copy-start(bf16[512,512]{1,0:T(8,128)(2,1)} %get-tuple-element.353) | copy-start | bytes 1572868
  804.5 9.8 %copy-start.11 = (bf16[512,2048]{0,1:T(8,128)(2,1)S(1)}, bf16[512,2048]{0,1:T(8,128)(2,1)}, u32[]{:S(2)}) copy-start(bf16[512,2048]{0,1:T(8,128)(2,1)} %get-tuple-element.360) | copy-start | bytes 6291460
  804.6 9.8 %copy-start.12 = (bf16[512,2048]{0,1:T(8,128)(2,1)S(1)}, bf16[512,2048]{0,1:T(8,128)(2,1)}, u32[]{:S(2)}) copy-start(bf16[512,2048]{0,1:T(8,128)(2,1)} %get-tuple-element.361) | copy-start | bytes 6291460
  804.6 9.8 %copy-start.13 = (bf16[512,2048]{0,1:T(8,128)(2,1)S(1)}, bf16[512,2048]{0,1:T(8,128)(2,1)}, u32[]{:S(2)}) copy-start(bf16[512,2048]{0,1:T(8,128)(2,1)} %get-tuple-element.362) | copy-start | bytes 6291460
  838.6 20.8 %copy-start.2 = (f32[1536,2048]{1,0:T(8,128)S(1)}, f32[1536,2048]{1,0:T(8,128)}, u32[]{:S(2)}) copy-start(f32[1536,2048]{1,0:T(8,128)} %fusion.59) | copy-start | bytes 37748740
  859.3 12.5 %copy-start.6 = (s32[512,64]{0,1:T(8,128)S(1)}, s32[512,64]{0,1:T(8,128)}, u32[]{:S(2)}) copy-start(s32[512,64]{0,1:T(8,128)} %copy-done.5) | copy-start | bytes 393220
  859.3 12.5 %copy-start.31 = (s32[64]{0:T(128)S(1)}, s32[64]{0:T(128)}, u32[]{:S(2)}) copy-start(s32[64]{0:T(128)} %copy-done.30) | copy-start | bytes 772
  859.3 12.5 %copy-start.34 = (pred[64]{0:T(512)(128)(4,1)S(1)}, pred[64]{0:T(512)(128)(4,1)}, u32[]{:S(2)}) copy-start(pred[64]{0:T(512)(128)(4,1)} %copy-done.33) | copy-start | bytes 196
  872.5 3.9 copy-start.1
  (1 other events, 0.5 us)
